TPU v7x, 256 devices: a whole 4x4x8 slice. The times are simulated.
256 devices in a mesh: shot: 8 (over x_hi, y), rcv: 32 (over x_lo, z, core).
Axes of the slice: x: 4 (x_hi: 2, x_lo: 2; x = x_hi * 2 + x_lo), y: 4, z: 8, core: 2. Of those that a mesh axis runs over, the one named last changes fastest.
Arguments:
- modeled: bfloat16 [2, 64, 8, 256, 512], P(None, 'shot', None, 'rcv'), may hold values from -9 to 9
- observed: bfloat16 [2, 8, 64, 256, 512], P(None, 'shot', 'rcv'), may hold values from -60 to 60
- mask: int32 [64, 8, 256], P('shot', None, 'rcv'), may hold values 0 or 1
- shot_order: int32 [64], replicated, may hold values from 0 to 63, as said below
- line_of_slot: int32 [8], replicated, may hold values from 0 to 7, as said below
- coupling: bfloat16 [2, 512, 512], replicated, may hold values from -0.25 to 0.25
- wavelet: float32 [2, 512], replicated, may hold values from -4 to 4
- damping: float32 [512], replicated, may hold values from 32768 to 524288
Outputs:
- new_wavelet: float32 [2, 512], replicated
- residual_out: bfloat16 [2, 64, 8, 256, 512], P(None, 'shot', None, 'rcv')
Inputs may be any that keep to these rules, and one draw needn't show every extreme that they name: Group g holds the shots shot_order[g * 8] to shot_order[(g + 1) * 8 - 1]; each shot number appears once. `line_of_slot`: each line appears in exactly one slot.
All inputs are finite; a program needn't handle non-finite values. No bound on the sum of `mask` on one device may be relied on, other than what follows from the above.
Results may differ from a plain program's by a relative error of at most 0.00045.
Values may be sent and summed in bfloat16 or wider, within the bound.
No kernel may reach another device: no remote copies, remote signals or barrier semaphores. Data moves between devices by JAX's collectives and lax.ppermute only.
A program may use at most 64 MiB of HBM per device.

v0:
```python
import jax
import jax.numpy as jnp
from jax import lax
from jax.sharding import PartitionSpec as P


def sent_to_all(array, axis):
    size = lax.axis_size(axis)
    return lax.all_to_all(
        jnp.broadcast_to(array[None], (size, *array.shape)), axis, 0, 0, tiled=True
    )


def of_everyone(array, axis):
    return sent_to_all(array, axis).sum(axis=0)


def in_one(arrays, axis):
    ends = [0]
    for a in arrays:
        ends.append(ends[-1] + a.size)
    subtotal = of_everyone(jnp.concatenate([a.ravel() for a in arrays]), axis)
    return tuple((subtotal[b:e].reshape(a.shape) for a, b, e in zip(arrays, ends, ends[1:])))


def weigh(trace, coupling):
    real_part = jnp.dot(trace[0], coupling[0], preferred_element_type=jnp.float32) - jnp.dot(
        trace[1], coupling[1], preferred_element_type=jnp.float32
    )
    imag_part = jnp.dot(trace[0], coupling[1], preferred_element_type=jnp.float32) + jnp.dot(
        trace[1], coupling[0], preferred_element_type=jnp.float32
    )
    return jnp.stack([real_part, imag_part])


def per_device(modeled, observed, mask, shot_order, line_of_slot, coupling, wavelet, damping):
    group_size = modeled.shape[1]
    line_count = modeled.shape[2]
    slot_count = lax.axis_size("shot")
    stored = observed[:, 0]
    spread = lax.all_to_all(stored, "rcv", split_axis=2, concat_axis=1, tiled=True)
    grouped = jnp.take(spread, shot_order, axis=1)
    grouped = grouped.reshape(2, slot_count, group_size, grouped.shape[2], grouped.shape[3])
    arrived = lax.all_to_all(grouped, "shot", split_axis=1, concat_axis=1, tiled=True)
    inverse = (
        jnp.zeros((line_count,), jnp.int32)
        .at[line_of_slot]
        .set(jnp.arange(line_count, dtype=jnp.int32))
    )
    by_line = jnp.transpose(jnp.take(arrived, inverse, axis=1), (0, 2, 1, 3, 4))
    wd = weigh(by_line, coupling)
    wg = weigh(modeled, coupling)
    live = mask.astype(jnp.float32)[..., None]
    res_re = live * (wd[0] - (wavelet[0] * wg[0] - wavelet[1] * wg[1]))
    res_im = live * (wd[1] - (wavelet[0] * wg[1] + wavelet[1] * wg[0]))
    num_re = jnp.sum(wg[0] * res_re + wg[1] * res_im, axis=(0, 1, 2))
    num_im = jnp.sum(wg[0] * res_im - wg[1] * res_re, axis=(0, 1, 2))
    den = jnp.sum(live * (wg[0] * wg[0] + wg[1] * wg[1]), axis=(0, 1, 2))
    numerator = jnp.stack([num_re, num_im])
    numerator, den = in_one((numerator, den), "rcv")
    numerator, den = in_one((numerator, den), "shot")
    new_wavelet = wavelet + numerator / (den + damping)[None, :]
    out_re = live * (wd[0] - (new_wavelet[0] * wg[0] - new_wavelet[1] * wg[1]))
    out_im = live * (wd[1] - (new_wavelet[0] * wg[1] + new_wavelet[1] * wg[0]))
    return (new_wavelet, jnp.stack([out_re, out_im]).astype(jnp.bfloat16))


def solution(mesh):
    placed = (
        P(None, "shot", None, "rcv", None),
        P(None, "shot", "rcv", None, None),
        P("shot", None, "rcv"),
        P(),
        P(),
        P(),
        P(),
        P(),
    )
    return jax.shard_map(
        per_device,
        mesh=mesh,
        in_specs=placed,
        out_specs=(P(), P(None, "shot", None, "rcv", None)),
        check_vma=False,
    )
```

profile of v0, /device:TPU:8, one launch (start us, length us, event | category | flops | bytes accessed | tf_op | source)
XLA Modules:
  0.0 104.6 jit_solution(12052726027214672724)
XLA Ops:
  0.6 3.3 %copy.49 = bf16[2,1,2,256,512]{4,2,0,3,1:T(2,128)(2,1)} copy(bf16[2,1,2,256,512]{4,3,2,1,0:T(8,128)(2,1)} %param.9) | data formatting | bytes 2097152 | tf_op args[1]
  3.9 9.9 %all-to-all-start = ((bf16[2,2,256,512]{3,1,0,2:T(2,128)(2,1)}), bf16[2,2,256,512]{3,1,0,2:T(2,128)(2,1)S(1)}, u32[]{:S(2)}, u32[]{:S(2)}) async-start(bf16[2,2,256,512]{3,1,0,2:T(2,128)(2,1)} %bitcast.74), calls=%async_computation | async-start | bytes 2097152 | tf_op jit(solution)/shard_map/all_to_all | solution.py:41
  14.0 0.6 copy-done.11
  14.6 0.6 scatter_custom_fusion
  15.3 0.6 copy-done.8
  15.9 26.4 %all-to-all-done = bf16[2,2,256,512]{3,1,0,2:T(2,128)(2,1)S(1)} async-done(((bf16[2,2,256,512]{3,1,0,2:T(2,128)(2,1)}), bf16[2,2,256,512]{3,1,0,2:T(2,128)(2,1)S(1)}, u32[]{:S(2)}, u32[]{:S(2)}) %all-to-all-start) | async-done | bytes 1048608 | tf_op jit(solution)/shard_map/all_to_all | solution.py:41
  42.3 0.2 copy.48
  42.5 0.1 copy.29
  42.6 0.6 gather_fusion
  43.3 1.1 %copy_select_fusion.1 = bf16[2,8,8,8,512]{4,3,2,0,1:T(8,128)(2,1)} fusion(bf16[2,8,8,8,512]{4,3,0,2,1:T(8,128)(2,1)S(1)} %bitcast.77, pred[8,8]{1,0:T(8,128)(4,1)S(1)} %broadcast_in_dim.43), kind=kLoop, calls=%fused_computation.10 | loop fusion | flops 524288 | bytes 2097216 | tf_op jit(solution)/shard_map/jit(_take)/select_n | solution.py:42
  44.4 7.2 %all-to-all-start.1 = ((bf16[2,8,8,8,512]{4,3,2,0,1:T(8,128)(2,1)}), bf16[2,8,8,8,512]{4,3,2,0,1:T(8,128)(2,1)S(1)}, u32[]{:S(2)}, u32[]{:S(2)}) async-start(bf16[2,8,8,8,512]{4,3,2,0,1:T(8,128)(2,1)} %copy_select_fusion.1), calls=%async_computation.1 | async-start | bytes 2097152 | tf_op jit(solution)/shard_map/all_to_all | solution.py:44
  51.7 1.4 %fusion.5 = f32[8,8,8,512]{3,2,1,0:T(8,128)} fusion(bf16[2,8,8,8,512]{4,3,2,1,0:T(8,128)(2,1)S(1)} %copy-done.4, bf16[2,512,512]{2,1,0:T(8,128)(2,1)S(1)} %copy-done), kind=kOutput, calls=%fused_computation.26 | convolution fusion | flops 268435456 | bytes 2097152 | tf_op jit(solution)/shard_map/dot_general | solution.py:30
  53.1 0.4 fusion.13
  53.5 1.4 %convolution_subtract_fusion.1 = f32[8,8,8,512]{3,2,1,0:T(8,128)} fusion(f32[8,8,8,512]{3,2,1,0:T(8,128)S(1)} %fusion.13, bf16[2,8,8,8,512]{4,3,2,1,0:T(8,128)(2,1)S(1)} %copy-done.4, bf16[2,512,512]{2,1,0:T(8,128)(2,1)S(1)} %copy-done), kind=kOutput, calls=%fused_computation.6 | convolution fusion | flops 268697600 | bytes 3145728 | tf_op jit(solution)/shard_map/dot_general | solution.py:27
  54.9 9.8 %all-to-all-done.1 = bf16[2,8,8,8,512]{4,3,2,0,1:T(8,128)(2,1)S(1)} async-done(((bf16[2,8,8,8,512]{4,3,2,0,1:T(8,128)(2,1)}), bf16[2,8,8,8,512]{4,3,2,0,1:T(8,128)(2,1)S(1)}, u32[]{:S(2)}, u32[]{:S(2)}) %all-to-all-start.1) | async-done | bytes 1048608 | tf_op jit(solution)/shard_map/all_to_all | solution.py:44
  64.8 0.6 gather_fusion.1
  65.4 0.2 fusion
  65.6 0.4 fusion.3
  66.0 0.4 fusion.11
  66.5 0.4 convolution_add_fusion
  66.9 0.4 convolution_subtract_fusion
  67.4 0.7 copy-done.1
  68.1 0.6 copy-done.5
  68.8 0.4 copy-done.6
  69.1 2.1 %add_reduce_fusion = (f32[512]{0:T(512)S(1)}, f32[512]{0:T(512)S(1)}, f32[512]{0:T(512)S(1)}, f32[8,8,8,512]{3,2,1,0:T(8,128)}) fusion(f32[8,8,8,512]{3,2,1,0:T(8,128)S(1)} %convolution_add_fusion, f32[8,8,8,512]{3,2,1,0:T(8,128)S(1)} %copy-done.1, f32[8,8,8,512]{3,2,1,0:T(8,128)S(1)} %convolution_subtract_fusion, f32[512]{0:T(512)S(1)} %bitcast.83, ...), kind=kOutput, calls=%fused_computation.17 | convolution fusion | flops 274725376 | bytes 6334464 | tf_op jit(solution)/shard_map/dot_general | solution.py:30
  71.4 16.8 %all_to_all.35 = f32[32,1,1536]{2,1,0:T(1,128)S(1)} all-to-all(f32[32,1,1536]{2,1,0:T(1,128)S(1)} %broadcast_in_dim.48), channel_id=1, replica_groups=mesh['shot'=8,'rcv'=32] {'rcv'}, dimensions={0} | all-to-all | bytes 393216 | tf_op jit(solution)/shard_map/all_to_all | solution.py:9
  88.2 0.1 reduce_sum.48
  88.4 12.1 %all_to_all.36 = f32[8,1,1536]{2,1,0:T(1,128)S(1)} all-to-all(f32[8,1,1536]{2,1,0:T(1,128)S(1)} %broadcast_in_dim.49), channel_id=1, replica_groups=mesh['shot'=8,'rcv'=32] {'shot'}, dimensions={0} | all-to-all | bytes 98304 | tf_op jit(solution)/shard_map/all_to_all | solution.py:9
  100.6 0.7 copy-done.10
  101.3 0.6 copy-done.9
  101.9 1.6 %fusion.1 = (bf16[1,8,8,8,512]{4,3,2,1,0:T(8,128)(2,1)S(1)}, bf16[1,8,8,8,512]{4,3,2,1,0:T(8,128)(2,1)S(1)}) fusion(f32[8,8,8,512]{3,2,1,0:T(8,128)S(1)} %copy-done.3, f32[8,8,8,512]{3,2,1,0:T(8,128)} %get-tuple-element.11, f32[8,8,8,512]{3,2,1,0:T(8,128)S(1)} %copy-done.1, f32[512]{0:T(512)S(1)} %bitcast.81, f32[512]{0:T(512)S(1)} %bitcast.80, ...), kind=kLoop, calls=%fused_computation.20 | loop fusion | flops 3145728 | bytes 5249024 | tf_op jit(solution)/shard_map/stack | solution.py:65
  103.5 1.1 %pad_maximum_fusion = bf16[2,8,8,8,512]{4,3,2,1,0:T(8,128)(2,1)} fusion(bf16[1,8,8,8,512]{4,3,2,1,0:T(8,128)(2,1)S(1)} %get-tuple-element.6, bf16[1,8,8,8,512]{4,3,2,1,0:T(8,128)(2,1)S(1)} %get-tuple-element.5), kind=kLoop, calls=%fused_computation.7 | loop fusion | flops 524288 | bytes 2097152 | tf_op jit(solution)/shard_map/stack | solution.py:65
  (42 shorter events, 0.5 us)
Async XLA Ops:
  3.9 9.9 %copy-start.12 = (s32[64]{0:T(128)S(1)}, s32[64]{0:T(128)}, u32[]{:S(2)}) copy-start(s32[64]{0:T(128)} %param.11) | copy-start | bytes 772
  3.9 10.0 %copy-start.7 = (s32[8,8,8]{2,1,0:T(8,128)S(1)}, s32[8,8,8]{2,1,0:T(8,128)}, u32[]{:S(2)}) copy-start(s32[8,8,8]{2,1,0:T(8,128)} %param.10) | copy-start | bytes 6148
  3.9 38.4 %all-to-all-start = ((bf16[2,2,256,512]{3,1,0,2:T(2,128)(2,1)}), bf16[2,2,256,512]{3,1,0,2:T(2,128)(2,1)S(1)}, u32[]{:S(2)}, u32[]{:S(2)}) async-start(bf16[2,2,256,512]{3,1,0,2:T(2,128)(2,1)} %bitcast.74), calls=%async_computation | async-start | bytes 2097152 | tf_op jit(solution)/shard_map/all_to_all | solution.py:41
  13.9 0.7 copy-start.11
  15.2 0.7 copy-start.8
  44.4 7.2 %copy-start = (bf16[2,512,512]{2,1,0:T(8,128)(2,1)S(1)}, bf16[2,512,512]{2,1,0:T(8,128)(2,1)}, u32[]{:S(2)}) copy-start(bf16[2,512,512]{2,1,0:T(8,128)(2,1)} %param.13) | copy-start | bytes 3145732
  44.4 7.2 %copy-start.4 = (bf16[2,8,8,8,512]{4,3,2,1,0:T(8,128)(2,1)S(1)}, bf16[2,8,8,8,512]{4,3,2,1,0:T(8,128)(2,1)}, u32[]{:S(2)}) copy-start(bf16[2,8,8,8,512]{4,3,2,1,0:T(8,128)(2,1)} %param.8) | copy-start | bytes 3145732
  44.4 20.3 %all-to-all-start.1 = ((bf16[2,8,8,8,512]{4,3,2,0,1:T(8,128)(2,1)}), bf16[2,8,8,8,512]{4,3,2,0,1:T(8,128)(2,1)S(1)}, u32[]{:S(2)}, u32[]{:S(2)}) async-start(bf16[2,8,8,8,512]{4,3,2,0,1:T(8,128)(2,1)} %copy_select_fusion.1), calls=%async_computation.1 | async-start | bytes 2097152 | tf_op jit(solution)/shard_map/all_to_all | solution.py:44
  66.9 1.2 %copy-start.1 = (f32[8,8,8,512]{3,2,1,0:T(8,128)S(1)}, f32[8,8,8,512]{3,2,1,0:T(8,128)}, u32[]{:S(2)}) copy-start(f32[8,8,8,512]{3,2,1,0:T(8,128)} %convolution_subtract_fusion.1) | copy-start | bytes 3145732
  66.9 1.9 %copy-start.5 = (bf16[2,8,8,8,512]{4,3,2,1,0:T(8,128)(2,1)S(1)}, bf16[2,8,8,8,512]{4,3,2,1,0:T(8,128)(2,1)}, u32[]{:S(2)}) copy-start(bf16[2,8,8,8,512]{4,3,2,1,0:T(8,128)(2,1)} %param.8) | copy-start | bytes 3145732
  66.9 2.2 %copy-start.6 = (f32[8,8,8,512]{3,2,1,0:T(8,128)S(1)}, f32[8,8,8,512]{3,2,1,0:T(8,128)}, u32[]{:S(2)}) copy-start(f32[8,8,8,512]{3,2,1,0:T(8,128)} %fusion.5) | copy-start | bytes 3145732
  67.4 3.9 %copy-start.2 = (f32[8,8,8,512]{3,2,1,0:T(8,128)}, f32[8,8,8,512]{3,2,1,0:T(8,128)S(1)}, u32[]{:S(2)}) copy-start(f32[8,8,8,512]{3,2,1,0:T(8,128)S(1)} %convolution_subtract_fusion) | copy-start | bytes 3145732
  71.3 30.6 %copy-start.3 = (f32[8,8,8,512]{3,2,1,0:T(8,128)S(1)}, f32[8,8,8,512]{3,2,1,0:T(8,128)}, u32[]{:S(2)}) copy-start(f32[8,8,8,512]{3,2,1,0:T(8,128)} %copy-done.2) | copy-start | bytes 3145732
  100.6 0.7 copy-start.10
  101.3 0.6 copy-start.9
where the time goes:
time: 105 us
  waiting for transfers between devices  36.1 us (34%)
  blocking collectives  28.9 us (28%)
  starting transfers between devices  17.1 us (16%)
  local copies, waits for them, and re-layouts  10.1 us (10%)
  matrix products  7.15 us (7%)
  other arithmetic  4.23 us (4%)
    all_to_all x2, blocking collectives, sent_to_all(): lax.all_to_all(jnp.broadcast_to(array[None], (size, *array.shape)), axis,...  28.9 us
    all_to_all x1, waiting for transfers between devices, per_device(): lax.all_to_all(stored, 'rcv', split_axis=2, concat_axis=1, tiled=True)  26.4 us
    all_to_all x1, starting transfers between devices, per_device(): lax.all_to_all(stored, 'rcv', split_axis=2, concat_axis=1, tiled=True)  9.91 us
    all_to_all x1, waiting for transfers between devices, per_device(): lax.all_to_all(grouped, 'shot', split_axis=1, concat_axis=1, tiled=True)  9.76 us
    unnamed x28, local copies, waits for them, and re-layouts  7.58 us
    all_to_all x1, starting transfers between devices, per_device(): lax.all_to_all(grouped, 'shot', split_axis=1, concat_axis=1, tiled=True)  7.21 us
    another operation x2, other arithmetic, per_device(): return (new_wavelet, jnp.stack([out_re, out_im]).astype(jnp.bfloat16))  2.7 us
    dot_general x2, matrix products, weigh(): jnp.dot(trace[1], coupling[0], preferred_element_type=jnp.float32)  2.58 us
  transfers between devices with their start and end apart: 2, of which 2 were waited for; matrix products, arithmetic and copies ran while one was open for 4% of the time, Pallas kernels for 0%

commit v1 on v0

--- a/solution.py
+++ b/solution.py
@@ -1,7 +1,19 @@
+import functools
 import jax
 import jax.numpy as jnp
 from jax import lax
 from jax.sharding import PartitionSpec as P
+
+
+def perform_fields(base_x, axis_tag, on_dim, dim_i):
+    state_now = lax.axis_size(axis_tag)
+    v1 = jnp.split(base_x, state_now, axis=on_dim)
+    fresh = jnp.stack(v1)
+    t1 = lax.all_to_all(fresh, axis_name=axis_tag, split_axis=0, concat_axis=0)
+    return jnp.concatenate(t1, axis=dim_i)
+
+
+spread_set = functools.partial(perform_fields, axis_tag="shot", on_dim=1, dim_i=1)
 
 
 def sent_to_all(array, axis):
@@ -41,7 +53,7 @@
     spread = lax.all_to_all(stored, "rcv", split_axis=2, concat_axis=1, tiled=True)
     grouped = jnp.take(spread, shot_order, axis=1)
     grouped = grouped.reshape(2, slot_count, group_size, grouped.shape[2], grouped.shape[3])
-    arrived = lax.all_to_all(grouped, "shot", split_axis=1, concat_axis=1, tiled=True)
+    arrived = spread_set(grouped)
     inverse = (
         jnp.zeros((line_count,), jnp.int32)
         .at[line_of_slot]

time: 105 us -> 109 us (1.038)
  local copies, waits for them, and re-layouts: 10.1 us -> 15.4 us
    unnamed x28 -> x35, local copies, waits for them, and re-layouts: 7.58 us -> 12.2 us
where the time goes in v1:
time: 109 us
  waiting for transfers between devices  36.1 us (33%)
  blocking collectives  28.9 us (27%)
  starting transfers between devices  17.1 us (16%)
  local copies, waits for them, and re-layouts  15.4 us (14%)
  matrix products  7.15 us (7%)
  other arithmetic  3.26 us (3%)
    all_to_all x2, blocking collectives, sent_to_all(): lax.all_to_all(jnp.broadcast_to(array[None], (size, *array.shape)), axis,...  28.9 us
    all_to_all x1, waiting for transfers between devices, per_device(): lax.all_to_all(stored, 'rcv', split_axis=2, concat_axis=1, tiled=True)  26.4 us
    unnamed x35, local copies, waits for them, and re-layouts  12.2 us
    all_to_all x1, starting transfers between devices, per_device(): lax.all_to_all(stored, 'rcv', split_axis=2, concat_axis=1, tiled=True)  9.91 us
    all_to_all x1, waiting for transfers between devices, perform_fields(): t1 = lax.all_to_all(fresh, axis_name=axis_tag, split_axis=0, concat_axis=0)  9.76 us
    all_to_all x1, starting transfers between devices, perform_fields(): t1 = lax.all_to_all(fresh, axis_name=axis_tag, split_axis=0, concat_axis=0)  7.21 us
    another operation x2, other arithmetic, per_device(): return (new_wavelet, jnp.stack([out_re, out_im]).astype(jnp.bfloat16))  2.7 us
    dot_general x2, matrix products, weigh(): jnp.dot(trace[1], coupling[0], preferred_element_type=jnp.float32)  2.58 us
  transfers between devices with their start and end apart: 2, of which 2 were waited for; matrix products, arithmetic and copies ran while one was open for 4% of the time, Pallas kernels for 0%

profile of v1, /device:TPU:8, one launch (start us, length us, event | category | flops | bytes accessed | tf_op | source)
XLA Modules:
  0.0 108.9 jit_solution(6524741617067389057)
XLA Ops:
  0.6 3.3 %copy.72 = bf16[2,1,2,256,512]{4,2,0,3,1:T(2,128)(2,1)} copy(bf16[2,1,2,256,512]{4,3,2,1,0:T(8,128)(2,1)} %param.9) | data formatting | bytes 2097152 | tf_op args[1]
  3.9 9.9 %all-to-all-start = ((bf16[2,2,256,512]{3,1,0,2:T(2,128)(2,1)}), bf16[2,2,256,512]{3,1,0,2:T(2,128)(2,1)S(1)}, u32[]{:S(2)}, u32[]{:S(2)}) async-start(bf16[2,2,256,512]{3,1,0,2:T(2,128)(2,1)} %bitcast.111), calls=%async_computation | async-start | bytes 2097152 | tf_op jit(solution)/shard_map/all_to_all | solution.py:53
  14.0 0.6 copy-done.11
  14.6 0.6 scatter_custom_fusion
  15.3 0.6 copy-done.8
  15.9 26.4 %all-to-all-done = bf16[2,2,256,512]{3,1,0,2:T(2,128)(2,1)S(1)} async-done(((bf16[2,2,256,512]{3,1,0,2:T(2,128)(2,1)}), bf16[2,2,256,512]{3,1,0,2:T(2,128)(2,1)S(1)}, u32[]{:S(2)}, u32[]{:S(2)}) %all-to-all-start) | async-done | bytes 1048608 | tf_op jit(solution)/shard_map/all_to_all | solution.py:53
  42.6 0.6 gather_fusion
  43.5 0.7 fusion.38
  44.1 0.7 fusion.37
  44.8 0.7 fusion.36
  45.4 0.7 fusion.35
  46.1 0.7 fusion.34
  46.8 0.7 fusion.33
  47.4 0.7 fusion.32
  48.1 0.7 fusion.31
  48.8 7.2 %all-to-all-start.1 = ((bf16[8,2,1,8,8,512]{5,4,3,1,2,0:T(8,128)(2,1)}), bf16[8,2,1,8,8,512]{5,4,3,1,2,0:T(8,128)(2,1)S(1)}, u32[]{:S(2)}, u32[]{:S(2)}) async-start(bf16[8,2,1,8,8,512]{5,4,3,1,2,0:T(8,128)(2,1)} %fusion.31), calls=%async_computation.1 | async-start | bytes 2097152 | tf_op jit(solution)/shard_map/all_to_all | solution.py:12
  56.0 1.4 %fusion.5 = f32[8,8,8,512]{3,2,1,0:T(8,128)} fusion(bf16[2,8,8,8,512]{4,3,2,1,0:T(8,128)(2,1)S(1)} %copy-done.4, bf16[2,512,512]{2,1,0:T(8,128)(2,1)S(1)} %copy-done), kind=kOutput, calls=%fused_computation.27 | convolution fusion | flops 268435456 | bytes 2097152 | tf_op jit(solution)/shard_map/dot_general | solution.py:42
  57.4 0.4 fusion.13
  57.9 1.4 %convolution_subtract_fusion.1 = f32[8,8,8,512]{3,2,1,0:T(8,128)} fusion(f32[8,8,8,512]{3,2,1,0:T(8,128)S(1)} %fusion.13, bf16[2,8,8,8,512]{4,3,2,1,0:T(8,128)(2,1)S(1)} %copy-done.4, bf16[2,512,512]{2,1,0:T(8,128)(2,1)S(1)} %copy-done), kind=kOutput, calls=%fused_computation.6 | convolution fusion | flops 268697600 | bytes 3145728 | tf_op jit(solution)/shard_map/dot_general | solution.py:39
  59.3 9.8 %all-to-all-done.1 = bf16[8,2,1,8,8,512]{5,4,3,1,2,0:T(8,128)(2,1)S(1)} async-done(((bf16[8,2,1,8,8,512]{5,4,3,1,2,0:T(8,128)(2,1)}), bf16[8,2,1,8,8,512]{5,4,3,1,2,0:T(8,128)(2,1)S(1)}, u32[]{:S(2)}, u32[]{:S(2)}) %all-to-all-start.1) | async-done | bytes 1048608 | tf_op jit(solution)/shard_map/all_to_all | solution.py:12
  69.1 0.6 gather_fusion.1
  70.8 0.4 convolution_add_fusion
  71.3 0.4 convolution_subtract_fusion
  71.7 0.7 copy-done.1
  72.5 0.7 copy-done.5
  73.5 2.1 %add_reduce_fusion = (f32[512]{0:T(512)S(1)}, f32[512]{0:T(512)S(1)}, f32[512]{0:T(512)S(1)}, f32[8,8,8,512]{3,2,1,0:T(8,128)}) fusion(f32[8,8,8,512]{3,2,1,0:T(8,128)S(1)} %convolution_add_fusion, f32[8,8,8,512]{3,2,1,0:T(8,128)S(1)} %copy-done.1, f32[8,8,8,512]{3,2,1,0:T(8,128)S(1)} %convolution_subtract_fusion, f32[512]{0:T(512)S(1)} %bitcast.121, ...), kind=kOutput, calls=%fused_computation.18 | convolution fusion | flops 274725376 | bytes 6334464 | tf_op jit(solution)/shard_map/dot_general | solution.py:42
  75.8 16.8 %all_to_all.35 = f32[32,1,1536]{2,1,0:T(1,128)S(1)} all-to-all(f32[32,1,1536]{2,1,0:T(1,128)S(1)} %broadcast_in_dim.48), channel_id=1, replica_groups=mesh['shot'=8,'rcv'=32] {'rcv'}, dimensions={0} | all-to-all | bytes 393216 | tf_op jit(solution)/shard_map/all_to_all | solution.py:21
  92.8 12.1 %all_to_all.36 = f32[8,1,1536]{2,1,0:T(1,128)S(1)} all-to-all(f32[8,1,1536]{2,1,0:T(1,128)S(1)} %broadcast_in_dim.49), channel_id=1, replica_groups=mesh['shot'=8,'rcv'=32] {'shot'}, dimensions={0} | all-to-all | bytes 98304 | tf_op jit(solution)/shard_map/all_to_all | solution.py:21
  105.0 0.7 copy-done.10
  105.7 0.6 copy-done.9
  106.2 1.6 %fusion.1 = (bf16[1,8,8,8,512]{4,3,2,1,0:T(8,128)(2,1)S(1)}, bf16[1,8,8,8,512]{4,3,2,1,0:T(8,128)(2,1)S(1)}) fusion(f32[8,8,8,512]{3,2,1,0:T(8,128)S(1)} %copy-done.3, f32[8,8,8,512]{3,2,1,0:T(8,128)} %get-tuple-element.11, f32[8,8,8,512]{3,2,1,0:T(8,128)S(1)} %copy-done.1, f32[512]{0:T(512)S(1)} %bitcast.119, f32[512]{0:T(512)S(1)} %bitcast.118, ...), kind=kLoop, calls=%fused_computation.21 | loop fusion | flops 3145728 | bytes 5249024 | tf_op jit(solution)/shard_map/stack | solution.py:77
  107.9 1.1 pad_maximum_fusion
  (50 shorter events, 2.5 us)
Async XLA Ops:
  3.9 9.9 %copy-start.12 = (s32[64]{0:T(128)S(1)}, s32[64]{0:T(128)}, u32[]{:S(2)}) copy-start(s32[64]{0:T(128)} %param.11) | copy-start | bytes 772
  3.9 10.0 %copy-start.7 = (s32[8,8,8]{2,1,0:T(8,128)S(1)}, s32[8,8,8]{2,1,0:T(8,128)}, u32[]{:S(2)}) copy-start(s32[8,8,8]{2,1,0:T(8,128)} %param.10) | copy-start | bytes 6148
  3.9 38.4 %all-to-all-start = ((bf16[2,2,256,512]{3,1,0,2:T(2,128)(2,1)}), bf16[2,2,256,512]{3,1,0,2:T(2,128)(2,1)S(1)}, u32[]{:S(2)}, u32[]{:S(2)}) async-start(bf16[2,2,256,512]{3,1,0,2:T(2,128)(2,1)} %bitcast.111), calls=%async_computation | async-start | bytes 2097152 | tf_op jit(solution)/shard_map/all_to_all | solution.py:53
  13.9 0.7 copy-start.11
  15.2 0.7 copy-start.8
  48.8 7.2 %copy-start = (bf16[2,512,512]{2,1,0:T(8,128)(2,1)S(1)}, bf16[2,512,512]{2,1,0:T(8,128)(2,1)}, u32[]{:S(2)}) copy-start(bf16[2,512,512]{2,1,0:T(8,128)(2,1)} %param.13) | copy-start | bytes 3145732
  48.8 7.2 %copy-start.4 = (bf16[2,8,8,8,512]{4,3,2,1,0:T(8,128)(2,1)S(1)}, bf16[2,8,8,8,512]{4,3,2,1,0:T(8,128)(2,1)}, u32[]{:S(2)}) copy-start(bf16[2,8,8,8,512]{4,3,2,1,0:T(8,128)(2,1)} %param.8) | copy-start | bytes 3145732
  48.8 20.3 %all-to-all-start.1 = ((bf16[8,2,1,8,8,512]{5,4,3,1,2,0:T(8,128)(2,1)}), bf16[8,2,1,8,8,512]{5,4,3,1,2,0:T(8,128)(2,1)S(1)}, u32[]{:S(2)}, u32[]{:S(2)}) async-start(bf16[8,2,1,8,8,512]{5,4,3,1,2,0:T(8,128)(2,1)} %fusion.31), calls=%async_computation.1 | async-start | bytes 2097152 | tf_op jit(solution)/shard_map/all_to_all | solution.py:12
  71.2 1.2 %copy-start.1 = (f32[8,8,8,512]{3,2,1,0:T(8,128)S(1)}, f32[8,8,8,512]{3,2,1,0:T(8,128)}, u32[]{:S(2)}) copy-start(f32[8,8,8,512]{3,2,1,0:T(8,128)} %convolution_subtract_fusion.1) | copy-start | bytes 3145732
  71.3 1.9 %copy-start.5 = (bf16[2,8,8,8,512]{4,3,2,1,0:T(8,128)(2,1)S(1)}, bf16[2,8,8,8,512]{4,3,2,1,0:T(8,128)(2,1)}, u32[]{:S(2)}) copy-start(bf16[2,8,8,8,512]{4,3,2,1,0:T(8,128)(2,1)} %param.8) | copy-start | bytes 3145732
  71.3 2.2 %copy-start.6 = (f32[8,8,8,512]{3,2,1,0:T(8,128)S(1)}, f32[8,8,8,512]{3,2,1,0:T(8,128)}, u32[]{:S(2)}) copy-start(f32[8,8,8,512]{3,2,1,0:T(8,128)} %fusion.5) | copy-start | bytes 3145732
  71.7 3.9 %copy-start.2 = (f32[8,8,8,512]{3,2,1,0:T(8,128)}, f32[8,8,8,512]{3,2,1,0:T(8,128)S(1)}, u32[]{:S(2)}) copy-start(f32[8,8,8,512]{3,2,1,0:T(8,128)S(1)} %convolution_subtract_fusion) | copy-start | bytes 3145732
  75.6 30.6 %copy-start.3 = (f32[8,8,8,512]{3,2,1,0:T(8,128)S(1)}, f32[8,8,8,512]{3,2,1,0:T(8,128)}, u32[]{:S(2)}) copy-start(f32[8,8,8,512]{3,2,1,0:T(8,128)} %copy-done.2) | copy-start | bytes 3145732
  104.9 0.7 copy-start.10
  105.6 0.6 copy-start.9
